TPU v7x, 512 devices: a whole 4x4x16 slice. The times are simulated.
512 devices in a mesh: surf: 128 (over z, y, core), pair: 4 (over x).
Axes of the slice: x: 4, y: 4, z: 16, core: 2. Of those that a mesh axis runs over, the one named last changes fastest.
Arguments:
- left_panel: bfloat16 [1024, 4, 128, 192], P(('surf', 'pair')), may hold values from -0.5 to 0.5
- right_panel: bfloat16 [1024, 4, 128, 192], P(('surf', 'pair')), may hold values from -6 to 6
- inverse: bfloat16 [1024, 128, 128], P(('surf', 'pair')), may hold values from -0.5 to 0.5
- target: int32 [1024, 4, 4], P(('surf', 'pair')), may hold values from 0 to 2047, as said below
- blocks: float32 [2048, 192, 192], P(('surf', 'pair')), may hold values from -12 to 12
- weights: bfloat16 [2048, 192, 512], P('surf', None, 'pair'), may hold values from -0.109375 to 0.109375
Outputs:
- updated: float32 [2048, 192, 192], P(('surf', 'pair'))
- coarse_panel: float32 [24576, 512], P('surf', 'pair')
Inputs may be any that keep to these rules, and one draw needn't show every extreme that they name: target[b, k, l] = target[b, l, k]. Pair block p lies on device p // 4 of the joined axes; the block of every term lies on a device with the same index along pair as the box's device, whose index along surf differs from the box's device's by at most 2 along the closed loop of 128 tiles. From the boxes of one device at most 8 unordered neighbour pairs (k <= l) go to any one tile, and every device sends exactly 8 to some tile in every draw.
All inputs are finite; a program needn't handle non-finite values.
Results may differ from a plain program's by a relative error of at most 0.0055.
Values may be sent and summed in bfloat16 or wider, within the bound.
A program may use at most 64 MiB of HBM per device.

v0:
```python
import jax
import jax.numpy as jnp
import numpy as np
from jax import lax
from jax.sharding import PartitionSpec as P

REACH = 2


def from_behind(shard, axis, by):
    count = lax.axis_size(axis)
    return lax.ppermute(shard, axis, [(i, (i + by) % count) for i in range(count)])


def in_order(tiles, dim):
    tiles = jnp.moveaxis(tiles, 0, dim)
    dims = tiles.shape
    return tiles.reshape(*dims[:dim], dims[dim] * dims[dim + 1], *dims[dim + 2 :])


def sent_to_all(shard, axis):
    copies = jnp.broadcast_to(shard, (lax.axis_size(axis), *shard.shape))
    return lax.all_to_all(copies, axis, split_axis=0, concat_axis=0, tiled=True)


def gathered_copies(shard, axis, dim):
    return in_order(sent_to_all(shard, axis), dim)


def unit_tables(neighbours):
    firsts = []
    seconds = []
    for first in range(neighbours):
        for second in range(first, neighbours):
            firsts.append(first)
            seconds.append(second)
    return (np.array(firsts, np.int32), np.array(seconds, np.int32))


def body(left_panel, right_panel, inverse, target, blocks, weights):
    box_count, neighbours, redundant, skeleton = left_panel.shape
    surf_count = lax.axis_size("surf")
    pair_count = lax.axis_size("pair")
    local_pairs = blocks.shape[0]
    spots = 2 * REACH + 1
    solved = jnp.einsum(
        "bij,bkjc->bkic", inverse, right_panel, preferred_element_type=jnp.float32
    ).astype(jnp.bfloat16)
    firsts, seconds = unit_tables(neighbours)
    per_box = firsts.shape[0]
    item_count = box_count * per_box
    unit_target = target[:, firsts, seconds].reshape(-1)
    dest_tile = unit_target // (local_pairs * pair_count)
    block_slot = unit_target % local_pairs
    relative = (dest_tile - lax.axis_index("surf") + surf_count) % surf_count
    spot = jnp.where(relative <= REACH, relative, relative - surf_count) + REACH
    products = (
        jnp.einsum("bkri,blrj->bklij", left_panel, solved, preferred_element_type=jnp.float32)
        .astype(jnp.bfloat16)
        .reshape(box_count * neighbours * neighbours, skeleton, skeleton)
    )
    item_box = jnp.arange(item_count, dtype=jnp.int32) // per_box
    item_first = jnp.tile(jnp.asarray(firsts), box_count)
    item_second = jnp.tile(jnp.asarray(seconds), box_count)
    direct_terms = products[(item_box * neighbours + item_first) * neighbours + item_second]
    swapped_terms = products[(item_box * neighbours + item_second) * neighbours + item_first]
    destination = spot * local_pairs + block_slot
    selector = jnp.arange(spots * local_pairs)[:, None] == destination[None, :]
    direct_pick = selector.astype(jnp.bfloat16)
    swapped_pick = (selector & (item_first != item_second)[None, :]).astype(jnp.bfloat16)
    grouped = jnp.einsum(
        "ps,sij->pij", direct_pick, direct_terms, preferred_element_type=jnp.float32
    )
    grouped = grouped + jnp.einsum(
        "ps,sji->pij", swapped_pick, swapped_terms, preferred_element_type=jnp.float32
    )
    grouped = grouped.reshape(spots, local_pairs, skeleton, skeleton)
    total = jnp.zeros((local_pairs, skeleton, skeleton), jnp.float32)
    for offset in range(-REACH, REACH + 1):
        piece = grouped[offset + REACH]
        if offset != 0:
            piece = from_behind(piece.astype(jnp.bfloat16), "surf", offset).astype(piece.dtype)
        total = total + piece
    updated = blocks - total
    rounded = updated.astype(jnp.bfloat16)
    coarse_panel = jnp.einsum(
        "pij,pjc->ic",
        gathered_copies(rounded, "pair", 0),
        weights,
        preferred_element_type=jnp.float32,
    )
    return (updated, coarse_panel)


def solution(mesh):
    in_specs = (
        P(("surf", "pair"), None, None, None),
        P(("surf", "pair"), None, None, None),
        P(("surf", "pair"), None, None),
        P(("surf", "pair"), None, None),
        P(("surf", "pair"), None, None),
        P("surf", None, "pair"),
    )
    out_specs = (P(("surf", "pair"), None, None), P("surf", "pair"))
    return jax.shard_map(body, mesh=mesh, in_specs=in_specs, out_specs=out_specs, check_vma=False)
```

profile of v0, /device:TPU:2, one launch (start us, length us, event | category | flops | bytes accessed | tf_op | source)
XLA Modules:
  0.0 85.8 jit_solution(10524643822154094715)
XLA Ops:
  0.6 0.0 copy-start
  0.6 0.7 tile.24
  1.4 0.1 ne.104
  1.5 0.7 tile.20
  2.1 0.1 tile.21
  2.2 0.7 tile.22
  2.9 0.1 tile.23
  3.0 0.8 copy.18
  3.7 0.8 gather_fusion
  4.5 0.1 copy.19
  4.6 0.1 reshape.205
  4.7 3.9 %convert_bitcast_fusion = bf16[2,4,4,192,192]{3,4,1,2,0:T(8,128)(2,1)} fusion(bf16[2,4,128,192]{2,3,1,0:T(8,128)(2,1)} %param.11, bf16[2,4,128,192]{2,3,1,0:T(8,128)(2,1)} %param.10, bf16[2,128,128]{2,1,0:T(8,128)(2,1)} %param.12), kind=kOutput, calls=%fused_computation.4 | convolution fusion | flops 353697792 | bytes 3211264 | tf_op jit(solution)/shard_map/bkri,blrj->bklij/dot_general | solution.py:58
  8.6 4.8 %copy.20 = bf16[2,4,4,192,192]{4,3,2,1,0:T(8,128)(2,1)} copy(bf16[2,4,4,192,192]{3,4,1,2,0:T(8,128)(2,1)} %convert_bitcast_fusion) | data formatting | bytes 4718592 | tf_op jit(solution)/shard_map/convert_element_type | solution.py:59
  13.5 4.0 %gather_fusion.2 = bf16[20,192,192]{2,1,0:T(8,128)(2,1)} fusion(bf16[32,192,192]{2,1,0:T(8,128)(2,1)} %bitcast.44, s32[1024]{0:T(1024)S(1)} %get-tuple-element.16), kind=kCustom, calls=%fused_computation.2 | custom fusion | bytes 2949200 | tf_op jit(solution)/shard_map/gather | solution.py:66
  17.4 2.6 %gather_fusion.1 = bf16[20,192,192]{2,1,0:T(8,128)(2,1)S(1)} fusion(bf16[32,192,192]{2,1,0:T(8,128)(2,1)} %bitcast.45, s32[1024]{0:T(1024)S(1)} %get-tuple-element.17), kind=kCustom, calls=%fused_computation.1 | custom fusion | bytes 2949200 | tf_op jit(solution)/shard_map/gather | solution.py:65
  20.0 4.7 %copy.30 = bf16[20,192,192]{1,0,2:T(8,128)(2,1)} copy(bf16[20,192,192]{2,1,0:T(8,128)(2,1)} %gather_fusion.2) | data formatting | bytes 2949120 | tf_op jit(solution)/shard_map/gather | solution.py:66
  24.8 2.4 %fusion.15 = f32[192,192,20]{0,2,1:T(8,128)S(1)} fusion(bf16[20,192,192]{1,0,2:T(8,128)(2,1)} %copy.30, s32[20]{0:T(128)S(1)} %fusion.20, pred[20]{0:T(512)(128)(4,1)S(1)} %ne.104), kind=kOutput, calls=%fused_computation.20 | convolution fusion | flops 29492000 | bytes 4423780 | tf_op jit(solution)/shard_map/ps,sji->pij/dot_general | solution.py:74
  27.2 1.8 %fusion.30 = (bf16[20,192,192]{2,0,1:T(8,128)(2,1)S(1)}, f32[20,192,192]{2,0,1:T(8,128)S(1)}) fusion(f32[192,192,20]{0,2,1:T(8,128)S(1)} %fusion.15, bf16[20,192,192]{2,1,0:T(8,128)(2,1)S(1)} %gather_fusion.1, s32[20]{0:T(128)S(1)} %fusion.20), kind=kOutput, calls=%fused_computation.51 | convolution fusion | flops 30966160 | bytes 8847440 | tf_op jit(solution)/shard_map/ps,sij->pij/dot_general | solution.py:71
  28.9 0.0 copy-start.1
  29.0 0.6 fusion.29
  29.5 13.9 %collective-permute-start = (bf16[4,192,192]{2,0,1:T(4,128)(2,1)S(1)}, bf16[4,192,192]{2,0,1:T(4,128)(2,1)S(1)}, u32[]{:S(2)}, u32[]{:S(2)}) collective-permute-start(bf16[4,192,192]{2,0,1:T(4,128)(2,1)S(1)} %get-tuple-element.8), channel_id=1, source_target_pairs={{0,504},{4,508},{8,0},{12,4},{16,8},{20,12},{24,16},{28,20},{32,24... | collective-permute-start | bytes 884744 | tf_op jit(solution)/shard_map/ppermute | solution.py:12
  43.4 1.9 %collective-permute-start.3 = (bf16[4,192,192]{2,0,1:T(4,128)(2,1)S(1)}, bf16[4,192,192]{2,0,1:T(4,128)(2,1)S(1)}, u32[]{:S(2)}, u32[]{:S(2)}) collective-permute-start(bf16[4,192,192]{2,0,1:T(4,128)(2,1)S(1)} %get-tuple-element.9), channel_id=1, source_target_pairs={{0,8},{4,12},{8,16},{12,20},{16,24},{20,28},{24,32},{28,36},{32,40... | collective-permute-start | bytes 884744 | tf_op jit(solution)/shard_map/ppermute | solution.py:12
  45.3 1.9 %collective-permute-start.2 = (bf16[4,192,192]{2,0,1:T(4,128)(2,1)S(1)}, bf16[4,192,192]{2,0,1:T(4,128)(2,1)S(1)}, u32[]{:S(2)}, u32[]{:S(2)}) collective-permute-start(bf16[4,192,192]{2,0,1:T(4,128)(2,1)S(1)} %get-tuple-element.10), channel_id=1, source_target_pairs={{0,4},{4,8},{8,12},{12,16},{16,20},{20,24},{24,28},{28,32},{32,36}... | collective-permute-start | bytes 884744 | tf_op jit(solution)/shard_map/ppermute | solution.py:12
  47.2 7.0 %collective-permute-start.1 = (bf16[4,192,192]{2,0,1:T(4,128)(2,1)S(1)}, bf16[4,192,192]{2,0,1:T(4,128)(2,1)S(1)}, u32[]{:S(2)}, u32[]{:S(2)}) collective-permute-start(bf16[4,192,192]{2,0,1:T(4,128)(2,1)S(1)} %get-tuple-element.11), channel_id=1, source_target_pairs={{0,508},{4,0},{8,4},{12,8},{16,12},{20,16},{24,20},{28,24},{32,28}... | collective-permute-start | bytes 884744 | tf_op jit(solution)/shard_map/ppermute | solution.py:12
  54.2 0.0 collective-permute-done
  54.2 6.4 %collective-permute-done.3 = bf16[4,192,192]{2,0,1:T(4,128)(2,1)S(1)} collective-permute-done((bf16[4,192,192]{2,0,1:T(4,128)(2,1)S(1)}, bf16[4,192,192]{2,0,1:T(4,128)(2,1)S(1)}, u32[]{:S(2)}, u32[]{:S(2)}) %collective-permute-start.3) | collective-permute-done | bytes 294944 | tf_op jit(solution)/shard_map/ppermute | solution.py:12
  60.6 2.8 %collective-permute-done.2 = bf16[4,192,192]{2,0,1:T(4,128)(2,1)S(1)} collective-permute-done((bf16[4,192,192]{2,0,1:T(4,128)(2,1)S(1)}, bf16[4,192,192]{2,0,1:T(4,128)(2,1)S(1)}, u32[]{:S(2)}, u32[]{:S(2)}) %collective-permute-start.2) | collective-permute-done | bytes 294944 | tf_op jit(solution)/shard_map/ppermute | solution.py:12
  63.4 0.0 collective-permute-done.1
  63.4 0.0 copy-done.1
  63.4 1.1 %fusion.27 = (bf16[4,192,192]{2,0,1:T(4,128)(2,1)S(1)}, f32[4,192,192]{2,0,1:T(4,128)S(1)}) fusion(bf16[4,192,192]{2,0,1:T(4,128)(2,1)S(1)} %collective-permute-done.3, bf16[4,192,192]{2,0,1:T(4,128)(2,1)S(1)} %collective-permute-done.2, f32[20,192,192]{2,0,1:T(8,128)S(1)} %get-tuple-element.15, bf16[4,192,192]{2,0,1:T(4,128)(2,1)S(1)} %collective-permute-done.1, ...), kind=kLoop, calls=%fused_computation.49 | loop fusion | flops 1474560 | bytes 3244032 | tf_op jit(solution)/shard_map/convert_element_type | solution.py:85
  64.5 1.3 %broadcast_in_dim.16 = bf16[4,4,192,192]{3,2,1,0:T(8,128)(2,1)} broadcast(bf16[4,192,192]{2,1,0:T(8,128)(2,1)S(1)} %copy.25), dimensions={1,2,3} | broadcast | bytes 1474560 | tf_op jit(solution)/shard_map/broadcast_in_dim | solution.py:22
  65.8 4.8 %all-to-all-start = ((bf16[4,4,192,192]{3,2,1,0:T(8,128)(2,1)}), bf16[4,4,192,192]{3,2,1,0:T(8,128)(2,1)S(1)}, u32[]{:S(2)}, u32[]{:S(2)}) async-start(bf16[4,4,192,192]{3,2,1,0:T(8,128)(2,1)} %broadcast_in_dim.16), calls=%async_computation | async-start | bytes 3145728 | tf_op jit(solution)/shard_map/all_to_all | solution.py:23
  70.7 1.0 %copy.26 = f32[4,192,192]{2,1,0:T(8,128)} copy(f32[4,192,192]{2,0,1:T(4,128)S(1)} %get-tuple-element.7) | data formatting | bytes 1179648
  71.7 13.0 %all-to-all-done = bf16[4,4,192,192]{3,2,1,0:T(8,128)(2,1)S(1)} async-done(((bf16[4,4,192,192]{3,2,1,0:T(8,128)(2,1)}), bf16[4,4,192,192]{3,2,1,0:T(8,128)(2,1)S(1)}, u32[]{:S(2)}, u32[]{:S(2)}) %all-to-all-start) | async-done | bytes 1179680 | tf_op jit(solution)/shard_map/all_to_all | solution.py:23
  84.7 0.0 copy-done
  84.7 1.2 %convolution_bitcast_fusion = f32[192,128]{1,0:T(8,128)} fusion(bf16[16,192,192]{2,1,0:T(8,128)(2,1)S(1)} %bitcast.46, bf16[16,192,128]{2,1,0:T(8,128)(2,1)S(1)} %copy-done), kind=kOutput, calls=%fused_computation.9 | convolution fusion | flops 150994944 | bytes 2064384 | tf_op jit(solution)/shard_map/pij,pjc->ic/dot_general | solution.py:86
  (4 shorter events, 0.1 us)
Async XLA Ops:
  0.6 84.1 %copy-start = (bf16[16,192,128]{2,1,0:T(8,128)(2,1)S(1)}, bf16[16,192,128]{2,1,0:T(8,128)(2,1)}, u32[]{:S(2)}) copy-start(bf16[16,192,128]{2,1,0:T(8,128)(2,1)} %param.15) | copy-start | bytes 2359300
  28.9 34.4 %copy-start.1 = (f32[4,192,192]{2,1,0:T(8,128)S(1)}, f32[4,192,192]{2,1,0:T(8,128)}, u32[]{:S(2)}) copy-start(f32[4,192,192]{2,1,0:T(8,128)} %param.14) | copy-start | bytes 1769476
  29.5 24.7 %collective-permute-start = (bf16[4,192,192]{2,0,1:T(4,128)(2,1)S(1)}, bf16[4,192,192]{2,0,1:T(4,128)(2,1)S(1)}, u32[]{:S(2)}, u32[]{:S(2)}) collective-permute-start(bf16[4,192,192]{2,0,1:T(4,128)(2,1)S(1)} %get-tuple-element.8), channel_id=1, source_target_pairs={{0,504},{4,508},{8,0},{12,4},{16,8},{20,12},{24,16},{28,20},{32,24... | collective-permute-start | bytes 884744 | tf_op jit(solution)/shard_map/ppermute | solution.py:12
  43.4 17.2 %collective-permute-start.3 = (bf16[4,192,192]{2,0,1:T(4,128)(2,1)S(1)}, bf16[4,192,192]{2,0,1:T(4,128)(2,1)S(1)}, u32[]{:S(2)}, u32[]{:S(2)}) collective-permute-start(bf16[4,192,192]{2,0,1:T(4,128)(2,1)S(1)} %get-tuple-element.9), channel_id=1, source_target_pairs={{0,8},{4,12},{8,16},{12,20},{16,24},{20,28},{24,32},{28,36},{32,40... | collective-permute-start | bytes 884744 | tf_op jit(solution)/shard_map/ppermute | solution.py:12
  45.3 18.1 %collective-permute-start.2 = (bf16[4,192,192]{2,0,1:T(4,128)(2,1)S(1)}, bf16[4,192,192]{2,0,1:T(4,128)(2,1)S(1)}, u32[]{:S(2)}, u32[]{:S(2)}) collective-permute-start(bf16[4,192,192]{2,0,1:T(4,128)(2,1)S(1)} %get-tuple-element.10), channel_id=1, source_target_pairs={{0,4},{4,8},{8,12},{12,16},{16,20},{20,24},{24,28},{28,32},{32,36}... | collective-permute-start | bytes 884744 | tf_op jit(solution)/shard_map/ppermute | solution.py:12
  47.2 16.1 %collective-permute-start.1 = (bf16[4,192,192]{2,0,1:T(4,128)(2,1)S(1)}, bf16[4,192,192]{2,0,1:T(4,128)(2,1)S(1)}, u32[]{:S(2)}, u32[]{:S(2)}) collective-permute-start(bf16[4,192,192]{2,0,1:T(4,128)(2,1)S(1)} %get-tuple-element.11), channel_id=1, source_target_pairs={{0,508},{4,0},{8,4},{12,8},{16,12},{20,16},{24,20},{28,24},{32,28}... | collective-permute-start | bytes 884744 | tf_op jit(solution)/shard_map/ppermute | solution.py:12
  65.8 18.8 %all-to-all-start = ((bf16[4,4,192,192]{3,2,1,0:T(8,128)(2,1)}), bf16[4,4,192,192]{3,2,1,0:T(8,128)(2,1)S(1)}, u32[]{:S(2)}, u32[]{:S(2)}) async-start(bf16[4,4,192,192]{3,2,1,0:T(8,128)(2,1)} %broadcast_in_dim.16), calls=%async_computation | async-start | bytes 3145728 | tf_op jit(solution)/shard_map/all_to_all | solution.py:23
where the time goes:
time: 86.5 us; the launch traced here: 85.8 us
  starting transfers between devices  29.5 us (34%)
  local copies, waits for them, and re-layouts  23.1 us (27%)
  waiting for transfers between devices  22.2 us (26%)
  matrix products  9.3 us (11%)
  other arithmetic  1.11 us (1%)
    ppermute x4, starting transfers between devices, from_behind(): lax.ppermute(shard, axis, [(i, (i + by) % count) for i in range(count)])  24.7 us
    all_to_all x1, waiting for transfers between devices, sent_to_all(): return lax.all_to_all(copies, axis, split_axis=0, concat_axis=0, tiled=True)  13 us
    ppermute x4, waiting for transfers between devices, from_behind(): lax.ppermute(shard, axis, [(i, (i + by) % count) for i in range(count)])  9.17 us
    gather x2, local copies, waits for them, and re-layouts, body(): products[(item_box * neighbours + item_second) * neighbours + item_first]  8.7 us
    all_to_all x1, starting transfers between devices, sent_to_all(): return lax.all_to_all(copies, axis, split_axis=0, concat_axis=0, tiled=True)  4.82 us
    convert_element_type x1, local copies, waits for them, and re-layouts, body(): products = jnp.einsum('bkri,blrj->bklij', left_panel, solved, preferred_e...  4.78 us
    dot_general x1, matrix products, body(): jnp.einsum('bkri,blrj->bklij', left_panel, solved, preferred_element_type...  3.94 us
    gather x1, local copies, waits for them, and re-layouts, body(): products[(item_box * neighbours + item_first) * neighbours + item_second]  2.56 us
  transfers between devices with their start and end apart: 5, of which 3 were waited for; matrix products, arithmetic and copies ran while one was open for 1% of the time, Pallas kernels for 0%

commit v1 on v0

v1 whole, which is shorter than its diff:
```python
import functools

import jax
import jax.numpy as jnp
from jax import lax
from jax.experimental import pallas as pl
from jax.experimental.pallas import tpu as pltpu
from jax.sharding import PartitionSpec as P

MESH = pl.DeviceIdType.MESH
REACH = 2
SPOTS = 2 * REACH + 1
CHUNKS = 3
RELAY, PARTNER, NEAR, FAR = 0, 1, 2, 3
SPOT_OF = {RELAY: 0, PARTNER: 1, NEAR: 3, FAR: 4}
OWN_SPOT = 2


def kernel(
    n_surf, n_pair, target, left, right, inverse, blocks, weights, updated, coarse,
    left_v, right_v, inverse_v, blocks_v, rows_a, cols_b, acc, index, pieces, arrived,
    weights_v, rounded, updated_v, part, part_in, coarse_v,
    load_sem, send_sem, recv_sem, wsend_sem, wrecv_sem, psend_sem, precv_sem, out_sem,
):
    boxes, neighbours, skeleton, redundant = left.shape
    local = blocks.shape[0]
    rows = skeleton // CHUNKS
    half = rows // 2
    packed = rows + half
    surf = lax.axis_index("surf")
    pair = lax.axis_index("pair")
    out = 2 * lax.rem(surf, 2) - 1

    def tile(offset):
        return lax.rem(surf + out * offset + n_surf, n_surf)

    def across(offset):
        return lax.rem(pair + offset, n_pair)

    barrier = pltpu.get_barrier_semaphore()
    for offset in (-1, 1, -2, 2):
        pl.semaphore_signal(barrier, inc=1, device_id=(tile(offset), pair), device_id_type=MESH)
    for offset in range(1, n_pair):
        pl.semaphore_signal(barrier, inc=1, device_id=(surf, across(offset)), device_id_type=MESH)

    loads = [
        pltpu.make_async_copy(source, into, load_sem.at[at])
        for at, (source, into) in enumerate(
            [
                (inverse, inverse_v),
                (right, right_v),
                (left, left_v),
                (weights.at[pl.ds(pair * local, local)], weights_v.at[0]),
                (blocks, blocks_v),
            ]
        )
    ]
    for load in loads:
        load.start()

    units = [(b, k, l) for b in range(boxes) for k in range(neighbours) for l in range(k, neighbours)]
    count = len(units)
    where_to = []
    for b, k, l in units:
        block = target[b, k, l]
        ahead = lax.rem(block // (local * n_pair) - surf + n_surf, n_surf)
        ahead = jnp.where(ahead <= REACH, ahead, ahead - n_surf)
        where_to.append((ahead * out + REACH) * local + lax.rem(block, local))
    for u in range(count):
        before = jnp.int32(count)
        for v in range(u):
            before = jnp.where(where_to[v] == where_to[u], v, before)
        index[u] = before
    for d in range(SPOTS * local):
        last = jnp.int32(count)
        for u in range(count):
            last = jnp.where(where_to[u] == d, u, last)
        index[count + d] = last

    acc[count] = jnp.zeros(acc.shape[1:], jnp.float32)

    pl.semaphore_wait(barrier, 3 + n_pair)

    wcopies = []
    for offset in (2, 1, 3):
        slot = n_pair - offset
        copy = pltpu.make_async_remote_copy(
            src_ref=weights.at[pl.ds(across(offset) * local, local)],
            dst_ref=weights_v.at[slot],
            send_sem=wsend_sem.at[slot - 1],
            recv_sem=wrecv_sem.at[slot - 1],
            device_id=(surf, across(offset)),
            device_id_type=MESH,
        )
        copy.start()
        wcopies.append(copy)

    for load in loads[:3]:
        load.wait()

    for b in range(boxes):
        solved = lax.dot_general(
            right_v[b].reshape(neighbours * skeleton, redundant),
            inverse_v[b],
            (((1,), (1,)), ((), ())),
            preferred_element_type=jnp.float32,
        ).astype(jnp.bfloat16)
        for k in range(neighbours):
            mine = solved[k * skeleton : (k + 1) * skeleton]
            panel = left_v[b, k]
            rows_a[b, k, :, :redundant] = panel
            rows_a[b, k, :, redundant:] = mine
            both = jnp.concatenate([mine, panel], axis=1)
            both = jnp.concatenate([both, both[redundant:]], axis=0)
            cols_b[b, k] = both.T

    lanes = lax.broadcasted_iota(jnp.int32, (half, 128), 1)
    for u, (b, k, l) in enumerate(units):
        if k == l:
            unit = jnp.dot(
                rows_a[b, k, :, :redundant], cols_b[b, l, :redundant], preferred_element_type=jnp.float32
            )
        else:
            unit = jnp.dot(rows_a[b, k], cols_b[b, l], preferred_element_type=jnp.float32)
        before = index[u]
        for r in range(CHUNKS):
            top = r * rows
            at = r * packed
            acc[u, at : at + rows] = unit[top : top + rows, :128] + acc[before, at : at + rows]
            tail = jnp.where(lanes < 64, unit[top : top + half, 128:], unit[top + half : top + rows, 128:])
            acc[u, at + rows : at + packed] = tail + acc[before, at + rows : at + packed]

    def piece_of(spot, slot, r):
        return acc[index[count + spot * local + slot], r * packed : (r + 1) * packed]

    to = {RELAY: -1, PARTNER: -1, NEAR: 1, FAR: 2}

    def send(kind, r):
        copy = pltpu.make_async_remote_copy(
            src_ref=pieces.at[kind, r],
            dst_ref=arrived.at[kind, r],
            send_sem=send_sem.at[kind, r],
            recv_sem=recv_sem.at[kind, r],
            device_id=(tile(to[kind]), pair),
            device_id_type=MESH,
        )
        copy.start()
        return copy

    copies = {}
    for r in range(CHUNKS):
        for kind in (RELAY, FAR, PARTNER):
            for slot in range(local):
                pieces[kind, r, slot] = piece_of(SPOT_OF[kind], slot, r).astype(jnp.bfloat16)
            copies[kind, r] = send(kind, r)
    for r in range(CHUNKS):
        copies[RELAY, r].wait_recv()
        for slot in range(local):
            joined = piece_of(SPOT_OF[NEAR], slot, r) + arrived[RELAY, r, slot].astype(jnp.float32)
            pieces[NEAR, r, slot] = joined.astype(jnp.bfloat16)
        copies[NEAR, r] = send(NEAR, r)

    loads[3].wait()
    loads[4].wait()
    pcopies = []
    outs = []
    own = []
    for r in range(CHUNKS):
        top = r * rows
        for kind in (PARTNER, FAR, NEAR):
            copies[kind, r].wait_recv()
        for slot in range(local):
            total = piece_of(OWN_SPOT, slot, r)
            for kind in (PARTNER, FAR, NEAR):
                total = total + arrived[kind, r, slot].astype(jnp.float32)
            tail = total[rows:]
            tail = jnp.concatenate([tail, pltpu.roll(tail, 64, axis=1)], axis=0)[:, :64]
            main = blocks_v[slot, top : top + rows, :128] - total[:rows]
            tail = blocks_v[slot, top : top + rows, 128:] - tail
            updated_v[slot, top : top + rows, :128] = main
            updated_v[slot, top : top + rows, 128:] = tail
            rounded[slot, :, :128] = main.astype(jnp.bfloat16)
            rounded[slot, :, 128:] = tail.astype(jnp.bfloat16)
        copy = pltpu.make_async_copy(
            updated_v.at[:, pl.ds(top, rows)], updated.at[:, pl.ds(top, rows)], out_sem.at[r]
        )
        copy.start()
        outs.append(copy)
        if r == 0:
            for copy in wcopies:
                copy.wait_recv()

        def panel_of(first, second):
            total = None
            for slot in range(local):
                both = jnp.concatenate([weights_v[first, slot], weights_v[second, slot]], axis=1)
                term = jnp.dot(rounded[slot], both, preferred_element_type=jnp.float32)
                total = term if total is None else total + term
            return total

        def send_part(offset, value):
            part[offset - 1, r] = value.astype(jnp.bfloat16)
            slot = n_pair - offset - 1
            copy = pltpu.make_async_remote_copy(
                src_ref=part.at[offset - 1, r],
                dst_ref=part_in.at[slot, r],
                send_sem=psend_sem.at[slot, r],
                recv_sem=precv_sem.at[slot, r],
                device_id=(surf, across(offset)),
                device_id_type=MESH,
            )
            copy.start()
            pcopies.append((r, copy))

        panel = panel_of(2, 1)
        send_part(2, panel[:, :128])
        send_part(1, panel[:, 128:])
        panel = panel_of(3, 0)
        send_part(3, panel[:, :128])
        coarse_v[top : top + rows] = panel[:, 128:]

    for r in range(CHUNKS):
        top = r * rows
        for at, copy in pcopies:
            if at == r:
                copy.wait_recv()
        total = coarse_v[top : top + rows]
        for slot in range(n_pair - 1):
            total = total + part_in[slot, r].astype(jnp.float32)
        coarse_v[top : top + rows] = total
    copy = pltpu.make_async_copy(coarse_v, coarse, out_sem.at[CHUNKS])
    copy.start()
    outs.append(copy)
    for copy in wcopies:
        copy.wait_send()
    for copy in copies.values():
        copy.wait_send()
    for _, copy in pcopies:
        copy.wait_send()
    for copy in outs:
        copy.wait()


def body(left, right, inverse, target, blocks, weights):
    n_surf = lax.axis_size("surf")
    n_pair = lax.axis_size("pair")
    boxes, neighbours, redundant, skeleton = left.shape
    local = blocks.shape[0]
    columns = weights.shape[2]
    packed = skeleton * 3 // 2 // CHUNKS
    rows = skeleton // CHUNKS
    count = boxes * neighbours * (neighbours + 1) // 2
    bf16, f32 = jnp.bfloat16, jnp.float32
    anywhere = pl.BlockSpec(memory_space=pl.ANY)
    dma = pltpu.SemaphoreType.DMA
    return pl.pallas_call(
        functools.partial(kernel, n_surf, n_pair),
        name="eliminate",
        out_shape=(
            jax.ShapeDtypeStruct(blocks.shape, f32),
            jax.ShapeDtypeStruct((skeleton, columns), f32),
        ),
        in_specs=[pl.BlockSpec(memory_space=pltpu.SMEM)] + [anywhere] * 5,
        out_specs=(anywhere, anywhere),
        scratch_shapes=[
            pltpu.VMEM((boxes, neighbours, skeleton, redundant), bf16),
            pltpu.VMEM((boxes, neighbours, skeleton, redundant), bf16),
            pltpu.VMEM(inverse.shape, bf16),
            pltpu.VMEM(blocks.shape, f32),
            pltpu.VMEM((boxes, neighbours, skeleton, 2 * redundant), bf16),
            pltpu.VMEM((boxes, neighbours, 2 * redundant, 256), bf16),
            pltpu.VMEM((count + 1, CHUNKS * packed, 128), f32),
            pltpu.SMEM((count + SPOTS * local,), jnp.int32),
            pltpu.VMEM((4, CHUNKS, local, packed, 128), bf16),
            pltpu.VMEM((4, CHUNKS, local, packed, 128), bf16),
            pltpu.VMEM((n_pair, local, skeleton, columns), bf16),
            pltpu.VMEM((local, rows, skeleton), bf16),
            pltpu.VMEM(blocks.shape, f32),
            pltpu.VMEM((n_pair - 1, CHUNKS, rows, columns), bf16),
            pltpu.VMEM((n_pair - 1, CHUNKS, rows, columns), bf16),
            pltpu.VMEM((skeleton, columns), f32),
            dma((5,)),
            dma((4, CHUNKS)),
            dma((4, CHUNKS)),
            dma((n_pair - 1,)),
            dma((n_pair - 1,)),
            dma((n_pair - 1, CHUNKS)),
            dma((n_pair - 1, CHUNKS)),
            dma((CHUNKS + 1,)),
        ],
        compiler_params=pltpu.CompilerParams(collective_id=0, has_side_effects=True),
    )(target, jnp.swapaxes(left, 2, 3), jnp.swapaxes(right, 2, 3), inverse, blocks, weights)


def solution(mesh):
    in_specs = (
        P(("surf", "pair"), None, None, None),
        P(("surf", "pair"), None, None, None),
        P(("surf", "pair"), None, None),
        P(("surf", "pair"), None, None),
        P(("surf", "pair"), None, None),
        P("surf", None, "pair"),
    )
    out_specs = (P(("surf", "pair"), None, None), P("surf", "pair"))
    return jax.shard_map(body, mesh=mesh, in_specs=in_specs, out_specs=out_specs, check_vma=False)
```

time: 86.5 us -> 33.8 us (0.39)
  the two profiles are of different devices: /device:TPU:2 before, /device:TPU:1 now
where the time goes in v1:
time: 33.8 us; the launch traced here: 33.6 us
  Pallas kernels  30.2 us (89%)
  local copies, waits for them, and re-layouts  2.74 us (8%)
  between operations  0.65 us (2%)
    pallas_call x1, Pallas kernels, body(): pl.pallas_call(functools.partial(kernel, n_surf, n_pair), name='eliminate...  30.2 us
    unnamed x4, local copies, waits for them, and re-layouts  2.74 us

profile of v1, /device:TPU:1, one launch (start us, length us, event | category | flops | bytes accessed | tf_op | source)
XLA Modules:
  0.0 33.6 jit_solution(9048458612373184770)
XLA Ops:
  0.6 30.2 %eliminate.1 = (f32[4,192,192]{2,1,0:T(8,128)}, f32[192,128]{1,0:T(8,128)}) custom-call(s32[2,4,4]{2,1,0:T(4,128)} %target.1, bf16[2,4,192,128]{3,2,1,0:T(8,128)(2,1)} %bitcast.2, bf16[2,4,192,128]{3,2,1,0:T(8,128)(2,1)} %bitcast.3, bf16[2,128,128]{2,1,0:T(8,128)(2,1)} %inverse.1, f32[4,192,192]{2,1,0:T(8,128)} %blocks.1, bf16[16,192,128]{2,1,0:T(8,128)(2,1)} %weights.1), custom_call_target="tpu_custom_call" | custom-call | tf_op jit(solution)/shard_map/eliminate/pallas_call | solution.py:256
  30.9 0.0 copy-start
  30.9 2.1 %copy.10 = f32[4,192,192]{2,1,0:T(8,128)} copy(f32[4,192,192]{2,1,0:T(8,128)} %get-tuple-element.4) | data formatting | bytes 1179648
  33.0 0.0 copy-done
  33.0 0.6 %copy.11 = f32[192,128]{1,0:T(8,128)} copy(f32[192,128]{1,0:T(8,128)S(1)} %copy-done) | data formatting | bytes 196608
Async XLA Ops:
  30.9 2.1 %copy-start = (f32[192,128]{1,0:T(8,128)S(1)}, f32[192,128]{1,0:T(8,128)}, u32[]{:S(2)}) copy-start(f32[192,128]{1,0:T(8,128)} %get-tuple-element.5) | copy-start | bytes 294916

commit v2 on v1

--- a/solution.py
+++ b/solution.py
@@ -18,9 +18,9 @@
 
 def kernel(
     n_surf, n_pair, target, left, right, inverse, blocks, weights, updated, coarse,
-    left_v, right_v, inverse_v, blocks_v, rows_a, cols_b, acc, index, pieces, arrived,
-    weights_v, rounded, updated_v, part, part_in, coarse_v,
-    load_sem, send_sem, recv_sem, wsend_sem, wrecv_sem, psend_sem, precv_sem, out_sem,
+    target_s, left_v, right_v, inverse_v, blocks_v, rows_a, cols_b, acc, index, pieces, arrived,
+    weights_v, rounded, part, part_in,
+    load_sem, send_sem, recv_sem, wsend_sem, wrecv_sem, psend_sem, precv_sem,
 ):
     boxes, neighbours, skeleton, redundant = left.shape
     local = blocks.shape[0]
@@ -38,15 +38,28 @@
         return lax.rem(pair + offset, n_pair)
 
     barrier = pltpu.get_barrier_semaphore()
-    for offset in (-1, 1, -2, 2):
-        pl.semaphore_signal(barrier, inc=1, device_id=(tile(offset), pair), device_id_type=MESH)
+    late = jnp.maximum(REACH - surf, 0)
+
+    def greet(closing):
+        for offset in range(-REACH, REACH + 1):
+            if offset != 0:
+                peer = surf + offset
+                closes = jnp.logical_or(peer < 0, peer >= n_surf)
+
+                @pl.when(closes if closing else jnp.logical_not(closes))
+                def _():
+                    there = lax.rem(peer + n_surf, n_surf)
+                    pl.semaphore_signal(barrier, inc=1, device_id=(there, pair), device_id_type=MESH)
+
     for offset in range(1, n_pair):
         pl.semaphore_signal(barrier, inc=1, device_id=(surf, across(offset)), device_id_type=MESH)
+    greet(False)
 
     loads = [
         pltpu.make_async_copy(source, into, load_sem.at[at])
         for at, (source, into) in enumerate(
             [
+                (target, target_s),
                 (inverse, inverse_v),
                 (right, right_v),
                 (left, left_v),
@@ -58,11 +71,14 @@
     for load in loads:
         load.start()
 
+    for load in loads[:4]:
+        load.wait()
+
     units = [(b, k, l) for b in range(boxes) for k in range(neighbours) for l in range(k, neighbours)]
     count = len(units)
     where_to = []
     for b, k, l in units:
-        block = target[b, k, l]
+        block = target_s[b, k, l]
         ahead = lax.rem(block // (local * n_pair) - surf + n_surf, n_surf)
         ahead = jnp.where(ahead <= REACH, ahead, ahead - n_surf)
         where_to.append((ahead * out + REACH) * local + lax.rem(block, local))
@@ -78,25 +94,6 @@
         index[count + d] = last
 
     acc[count] = jnp.zeros(acc.shape[1:], jnp.float32)
-
-    pl.semaphore_wait(barrier, 3 + n_pair)
-
-    wcopies = []
-    for offset in (2, 1, 3):
-        slot = n_pair - offset
-        copy = pltpu.make_async_remote_copy(
-            src_ref=weights.at[pl.ds(across(offset) * local, local)],
-            dst_ref=weights_v.at[slot],
-            send_sem=wsend_sem.at[slot - 1],
-            recv_sem=wrecv_sem.at[slot - 1],
-            device_id=(surf, across(offset)),
-            device_id_type=MESH,
-        )
-        copy.start()
-        wcopies.append(copy)
-
-    for load in loads[:3]:
-        load.wait()
 
     for b in range(boxes):
         solved = lax.dot_general(
@@ -130,6 +127,23 @@
             tail = jnp.where(lanes < 64, unit[top : top + half, 128:], unit[top + half : top + rows, 128:])
             acc[u, at + rows : at + packed] = tail + acc[before, at + rows : at + packed]
 
+    pl.semaphore_wait(barrier, 2 * REACH + n_pair - 1 - late)
+    greet(True)
+
+    wcopies = []
+    for offset in (2, 1, 3):
+        slot = n_pair - offset
+        copy = pltpu.make_async_remote_copy(
+            src_ref=weights.at[pl.ds(across(offset) * local, local)],
+            dst_ref=weights_v.at[slot],
+            send_sem=wsend_sem.at[slot - 1],
+            recv_sem=wrecv_sem.at[slot - 1],
+            device_id=(surf, across(offset)),
+            device_id_type=MESH,
+        )
+        copy.start()
+        wcopies.append(copy)
+
     def piece_of(spot, slot, r):
         return acc[index[count + spot * local + slot], r * packed : (r + 1) * packed]
 
@@ -148,8 +162,13 @@
         return copy
 
     copies = {}
-    for r in range(CHUNKS):
-        for kind in (RELAY, FAR, PARTNER):
+    for kind in (RELAY, PARTNER, FAR):
+        if kind == FAR:
+            @pl.when(surf == 0)
+            def _():
+                pl.semaphore_wait(barrier, REACH)
+
+        for r in range(CHUNKS):
             for slot in range(local):
                 pieces[kind, r, slot] = piece_of(SPOT_OF[kind], slot, r).astype(jnp.bfloat16)
             copies[kind, r] = send(kind, r)
@@ -160,10 +179,9 @@
             pieces[NEAR, r, slot] = joined.astype(jnp.bfloat16)
         copies[NEAR, r] = send(NEAR, r)
 
-    loads[3].wait()
     loads[4].wait()
+    loads[5].wait()
     pcopies = []
-    outs = []
     own = []
     for r in range(CHUNKS):
         top = r * rows
@@ -177,15 +195,10 @@
             tail = jnp.concatenate([tail, pltpu.roll(tail, 64, axis=1)], axis=0)[:, :64]
             main = blocks_v[slot, top : top + rows, :128] - total[:rows]
             tail = blocks_v[slot, top : top + rows, 128:] - tail
-            updated_v[slot, top : top + rows, :128] = main
-            updated_v[slot, top : top + rows, 128:] = tail
+            updated[slot, top : top + rows, :128] = main
+            updated[slot, top : top + rows, 128:] = tail
             rounded[slot, :, :128] = main.astype(jnp.bfloat16)
             rounded[slot, :, 128:] = tail.astype(jnp.bfloat16)
-        copy = pltpu.make_async_copy(
-            updated_v.at[:, pl.ds(top, rows)], updated.at[:, pl.ds(top, rows)], out_sem.at[r]
-        )
-        copy.start()
-        outs.append(copy)
         if r == 0:
             for copy in wcopies:
                 copy.wait_recv()
@@ -217,28 +230,27 @@
         send_part(1, panel[:, 128:])
         panel = panel_of(3, 0)
         send_part(3, panel[:, :128])
-        coarse_v[top : top + rows] = panel[:, 128:]
+        coarse[top : top + rows] = panel[:, 128:]
 
     for r in range(CHUNKS):
         top = r * rows
         for at, copy in pcopies:
             if at == r:
                 copy.wait_recv()
-        total = coarse_v[top : top + rows]
+        total = coarse[top : top + rows]
         for slot in range(n_pair - 1):
             total = total + part_in[slot, r].astype(jnp.float32)
-        coarse_v[top : top + rows] = total
-    copy = pltpu.make_async_copy(coarse_v, coarse, out_sem.at[CHUNKS])
-    copy.start()
-    outs.append(copy)
+        coarse[top : top + rows] = total
+    @pl.when(surf == 1)
+    def _():
+        pl.semaphore_wait(barrier, 1)
+
     for copy in wcopies:
         copy.wait_send()
     for copy in copies.values():
         copy.wait_send()
     for _, copy in pcopies:
         copy.wait_send()
-    for copy in outs:
-        copy.wait()
 
 
 def body(left, right, inverse, target, blocks, weights):
@@ -252,17 +264,19 @@
     count = boxes * neighbours * (neighbours + 1) // 2
     bf16, f32 = jnp.bfloat16, jnp.float32
     anywhere = pl.BlockSpec(memory_space=pl.ANY)
+    on_chip = pl.BlockSpec(memory_space=pltpu.VMEM)
     dma = pltpu.SemaphoreType.DMA
     return pl.pallas_call(
         functools.partial(kernel, n_surf, n_pair),
         name="eliminate",
         out_shape=(
-            jax.ShapeDtypeStruct(blocks.shape, f32),
-            jax.ShapeDtypeStruct((skeleton, columns), f32),
+            pltpu.VMEM(blocks.shape, f32),
+            pltpu.VMEM((skeleton, columns), f32),
         ),
-        in_specs=[pl.BlockSpec(memory_space=pltpu.SMEM)] + [anywhere] * 5,
-        out_specs=(anywhere, anywhere),
+        in_specs=[anywhere] * 6,
+        out_specs=(on_chip, on_chip),
         scratch_shapes=[
+            pltpu.SMEM((boxes, neighbours, neighbours), jnp.int32),
             pltpu.VMEM((boxes, neighbours, skeleton, redundant), bf16),
             pltpu.VMEM((boxes, neighbours, skeleton, redundant), bf16),
             pltpu.VMEM(inverse.shape, bf16),
@@ -275,20 +289,17 @@
             pltpu.VMEM((4, CHUNKS, local, packed, 128), bf16),
             pltpu.VMEM((n_pair, local, skeleton, columns), bf16),
             pltpu.VMEM((local, rows, skeleton), bf16),
-            pltpu.VMEM(blocks.shape, f32),
             pltpu.VMEM((n_pair - 1, CHUNKS, rows, columns), bf16),
             pltpu.VMEM((n_pair - 1, CHUNKS, rows, columns), bf16),
-            pltpu.VMEM((skeleton, columns), f32),
-            dma((5,)),
+            dma((6,)),
             dma((4, CHUNKS)),
             dma((4, CHUNKS)),
             dma((n_pair - 1,)),
             dma((n_pair - 1,)),
             dma((n_pair - 1, CHUNKS)),
             dma((n_pair - 1, CHUNKS)),
-            dma((CHUNKS + 1,)),
         ],
-        compiler_params=pltpu.CompilerParams(collective_id=0, has_side_effects=True),
+        compiler_params=pltpu.CompilerParams(collective_id=0, has_side_effects=True, vmem_limit_bytes=66048000),
     )(target, jnp.swapaxes(left, 2, 3), jnp.swapaxes(right, 2, 3), inverse, blocks, weights)
 
 

time: 33.8 us -> 29.3 us (0.87)
  the two profiles are of different devices: /device:TPU:1 before, /device:TPU:2 now
where the time goes in v2:
time: 29.3 us; the launch traced here: 29.1 us
  Pallas kernels  27 us (92%)
  local copies, waits for them, and re-layouts  1.52 us (5%)
  between operations  0.64 us (2%)
    pallas_call x1, Pallas kernels, body(): pl.pallas_call(functools.partial(kernel, n_surf, n_pair), name='eliminate...  27 us
    unnamed x2, local copies, waits for them, and re-layouts  1.52 us

profile of v2, /device:TPU:2, one launch (start us, length us, event | category | flops | bytes accessed | tf_op | source)
XLA Modules:
  0.0 29.1 jit_solution(6800016727245745527)
XLA Ops:
  0.6 27.0 %eliminate.1 = (f32[4,192,192]{2,1,0:T(8,128)S(1)}, f32[192,128]{1,0:T(8,128)S(1)}) custom-call(s32[2,4,4]{2,1,0:T(4,128)} %target.1, bf16[2,4,192,128]{3,2,1,0:T(8,128)(2,1)} %bitcast.2, bf16[2,4,192,128]{3,2,1,0:T(8,128)(2,1)} %bitcast.3, bf16[2,128,128]{2,1,0:T(8,128)(2,1)} %inverse.1, f32[4,192,192]{2,1,0:T(8,128)} %blocks.1, bf16[16,192,128]{2,1,0:T(8,128)(2,1)} %weights.1), custom_call_target="tpu_custom_call" | custom-call | tf_op jit(solution)/shard_map/eliminate/pallas_call | solution.py:269
  27.6 0.9 %copy.10 = f32[4,192,192]{2,1,0:T(8,128)} copy(f32[4,192,192]{2,1,0:T(8,128)S(1)} %get-tuple-element.2) | data formatting | bytes 1179648
  28.5 0.6 %copy.11 = f32[192,128]{1,0:T(8,128)} copy(f32[192,128]{1,0:T(8,128)S(1)} %get-tuple-element.3) | data formatting | bytes 196608

commit v3 on v2

--- a/solution.py
+++ b/solution.py
@@ -11,6 +11,7 @@
 REACH = 2
 SPOTS = 2 * REACH + 1
 CHUNKS = 3
+VMEM = 66048000
 RELAY, PARTNER, NEAR, FAR = 0, 1, 2, 3
 SPOT_OF = {RELAY: 0, PARTNER: 1, NEAR: 3, FAR: 4}
 OWN_SPOT = 2
@@ -19,8 +20,8 @@
 def kernel(
     n_surf, n_pair, target, left, right, inverse, blocks, weights, updated, coarse,
     target_s, left_v, right_v, inverse_v, blocks_v, rows_a, cols_b, acc, index, pieces, arrived,
-    weights_v, rounded, part, part_in,
-    load_sem, send_sem, recv_sem, wsend_sem, wrecv_sem, psend_sem, precv_sem,
+    weights_own, weights_in, rounded, part, part_in,
+    load_sem, send_sem, partner_sem, recv_sem, wsend_sem, wrecv_sem, psend_sem, precv_sem,
 ):
     boxes, neighbours, skeleton, redundant = left.shape
     local = blocks.shape[0]
@@ -37,24 +38,6 @@
     def across(offset):
         return lax.rem(pair + offset, n_pair)
 
-    barrier = pltpu.get_barrier_semaphore()
-    late = jnp.maximum(REACH - surf, 0)
-
-    def greet(closing):
-        for offset in range(-REACH, REACH + 1):
-            if offset != 0:
-                peer = surf + offset
-                closes = jnp.logical_or(peer < 0, peer >= n_surf)
-
-                @pl.when(closes if closing else jnp.logical_not(closes))
-                def _():
-                    there = lax.rem(peer + n_surf, n_surf)
-                    pl.semaphore_signal(barrier, inc=1, device_id=(there, pair), device_id_type=MESH)
-
-    for offset in range(1, n_pair):
-        pl.semaphore_signal(barrier, inc=1, device_id=(surf, across(offset)), device_id_type=MESH)
-    greet(False)
-
     loads = [
         pltpu.make_async_copy(source, into, load_sem.at[at])
         for at, (source, into) in enumerate(
@@ -63,13 +46,31 @@
                 (inverse, inverse_v),
                 (right, right_v),
                 (left, left_v),
-                (weights.at[pl.ds(pair * local, local)], weights_v.at[0]),
+                (weights.at[pl.ds(pair * local, local)], weights_own),
                 (blocks, blocks_v),
             ]
         )
     ]
     for load in loads:
         load.start()
+
+    barrier = pltpu.get_barrier_semaphore()
+    late = jnp.maximum(REACH - surf, 0)
+
+    def greet(closing):
+        for offset in range(-REACH, REACH + 1):
+            if offset != 0:
+                peer = surf + offset
+                closes = jnp.logical_or(peer < 0, peer >= n_surf)
+
+                @pl.when(closes if closing else jnp.logical_not(closes))
+                def _():
+                    there = lax.rem(peer + n_surf, n_surf)
+                    pl.semaphore_signal(barrier, inc=1, device_id=(there, pair), device_id_type=MESH)
+
+    for offset in range(1, n_pair):
+        pl.semaphore_signal(barrier, inc=1, device_id=(surf, across(offset)), device_id_type=MESH)
+    greet(False)
 
     for load in loads[:4]:
         load.wait()
@@ -130,31 +131,39 @@
     pl.semaphore_wait(barrier, 2 * REACH + n_pair - 1 - late)
     greet(True)
 
-    wcopies = []
     for offset in (2, 1, 3):
         slot = n_pair - offset
         copy = pltpu.make_async_remote_copy(
             src_ref=weights.at[pl.ds(across(offset) * local, local)],
-            dst_ref=weights_v.at[slot],
-            send_sem=wsend_sem.at[slot - 1],
-            recv_sem=wrecv_sem.at[slot - 1],
+            dst_ref=weights_in.at[pl.ds((slot - 1) * local, local)],
+            send_sem=wsend_sem,
+            recv_sem=wrecv_sem,
             device_id=(surf, across(offset)),
             device_id_type=MESH,
         )
         copy.start()
-        wcopies.append(copy)
 
     def piece_of(spot, slot, r):
         return acc[index[count + spot * local + slot], r * packed : (r + 1) * packed]
 
     to = {RELAY: -1, PARTNER: -1, NEAR: 1, FAR: 2}
+
+    def all_sent(source, into, sem):
+        pltpu.make_async_remote_copy(
+            src_ref=source, dst_ref=into, send_sem=sem, recv_sem=sem, device_id=(surf, across(1)), device_id_type=MESH
+        ).wait_send()
+
+    def all_in(source, into, sem):
+        pltpu.make_async_remote_copy(
+            src_ref=source, dst_ref=into, send_sem=sem, recv_sem=sem, device_id=(surf, across(1)), device_id_type=MESH
+        ).wait_recv()
 
     def send(kind, r):
         copy = pltpu.make_async_remote_copy(
             src_ref=pieces.at[kind, r],
             dst_ref=arrived.at[kind, r],
-            send_sem=send_sem.at[kind, r],
-            recv_sem=recv_sem.at[kind, r],
+            send_sem=send_sem,
+            recv_sem=partner_sem if kind == PARTNER else recv_sem.at[kind, r],
             device_id=(tile(to[kind]), pair),
             device_id_type=MESH,
         )
@@ -181,11 +190,12 @@
 
     loads[4].wait()
     loads[5].wait()
-    pcopies = []
     own = []
     for r in range(CHUNKS):
         top = r * rows
-        for kind in (PARTNER, FAR, NEAR):
+        if r == 0:
+            all_in(pieces.at[PARTNER], arrived.at[PARTNER], partner_sem)
+        for kind in (FAR, NEAR):
             copies[kind, r].wait_recv()
         for slot in range(local):
             total = piece_of(OWN_SPOT, slot, r)
@@ -200,13 +210,15 @@
             rounded[slot, :, :128] = main.astype(jnp.bfloat16)
             rounded[slot, :, 128:] = tail.astype(jnp.bfloat16)
         if r == 0:
-            for copy in wcopies:
-                copy.wait_recv()
+            all_in(weights.at[pl.ds(0, (n_pair - 1) * local)], weights_in, wrecv_sem)
+
+        def weights_of(offset, slot):
+            return weights_own[slot] if offset == 0 else weights_in[(offset - 1) * local + slot]
 
         def panel_of(first, second):
             total = None
             for slot in range(local):
-                both = jnp.concatenate([weights_v[first, slot], weights_v[second, slot]], axis=1)
+                both = jnp.concatenate([weights_of(first, slot), weights_of(second, slot)], axis=1)
                 term = jnp.dot(rounded[slot], both, preferred_element_type=jnp.float32)
                 total = term if total is None else total + term
             return total
@@ -217,13 +229,12 @@
             copy = pltpu.make_async_remote_copy(
                 src_ref=part.at[offset - 1, r],
                 dst_ref=part_in.at[slot, r],
-                send_sem=psend_sem.at[slot, r],
-                recv_sem=precv_sem.at[slot, r],
+                send_sem=psend_sem,
+                recv_sem=precv_sem,
                 device_id=(surf, across(offset)),
                 device_id_type=MESH,
             )
             copy.start()
-            pcopies.append((r, copy))
 
         panel = panel_of(2, 1)
         send_part(2, panel[:, :128])
@@ -232,25 +243,32 @@
         send_part(3, panel[:, :128])
         coarse[top : top + rows] = panel[:, 128:]
 
+    all_in(part, part_in, precv_sem)
     for r in range(CHUNKS):
         top = r * rows
-        for at, copy in pcopies:
-            if at == r:
-                copy.wait_recv()
         total = coarse[top : top + rows]
         for slot in range(n_pair - 1):
             total = total + part_in[slot, r].astype(jnp.float32)
         coarse[top : top + rows] = total
+
     @pl.when(surf == 1)
     def _():
         pl.semaphore_wait(barrier, 1)
 
-    for copy in wcopies:
-        copy.wait_send()
-    for copy in copies.values():
-        copy.wait_send()
-    for _, copy in pcopies:
-        copy.wait_send()
+    all_sent(weights.at[pl.ds(0, (n_pair - 1) * local)], weights_in, wsend_sem)
+    all_sent(pieces, arrived, send_sem)
+    all_sent(part, part_in, psend_sem)
+
+
+def store(updated, coarse, updated_out, coarse_out, sem):
+    copies = [
+        pltpu.make_async_copy(updated, updated_out, sem.at[0]),
+        pltpu.make_async_copy(coarse, coarse_out, sem.at[1]),
+    ]
+    for copy in copies:
+        copy.start()
+    for copy in copies:
+        copy.wait()
 
 
 def body(left, right, inverse, target, blocks, weights):
@@ -266,7 +284,7 @@
     anywhere = pl.BlockSpec(memory_space=pl.ANY)
     on_chip = pl.BlockSpec(memory_space=pltpu.VMEM)
     dma = pltpu.SemaphoreType.DMA
-    return pl.pallas_call(
+    updated, panel = pl.pallas_call(
         functools.partial(kernel, n_surf, n_pair),
         name="eliminate",
         out_shape=(
@@ -287,20 +305,34 @@
             pltpu.SMEM((count + SPOTS * local,), jnp.int32),
             pltpu.VMEM((4, CHUNKS, local, packed, 128), bf16),
             pltpu.VMEM((4, CHUNKS, local, packed, 128), bf16),
-            pltpu.VMEM((n_pair, local, skeleton, columns), bf16),
+            pltpu.VMEM((local, skeleton, columns), bf16),
+            pltpu.VMEM(((n_pair - 1) * local, skeleton, columns), bf16),
             pltpu.VMEM((local, rows, skeleton), bf16),
             pltpu.VMEM((n_pair - 1, CHUNKS, rows, columns), bf16),
             pltpu.VMEM((n_pair - 1, CHUNKS, rows, columns), bf16),
             dma((6,)),
+            dma,
+            dma,
             dma((4, CHUNKS)),
-            dma((4, CHUNKS)),
-            dma((n_pair - 1,)),
-            dma((n_pair - 1,)),
-            dma((n_pair - 1, CHUNKS)),
-            dma((n_pair - 1, CHUNKS)),
+            dma,
+            dma,
+            dma,
+            dma,
         ],
-        compiler_params=pltpu.CompilerParams(collective_id=0, has_side_effects=True, vmem_limit_bytes=66048000),
+        compiler_params=pltpu.CompilerParams(collective_id=0, has_side_effects=True, vmem_limit_bytes=VMEM),
     )(target, jnp.swapaxes(left, 2, 3), jnp.swapaxes(right, 2, 3), inverse, blocks, weights)
+    return pl.pallas_call(
+        store,
+        name="store",
+        out_shape=(
+            jax.ShapeDtypeStruct(blocks.shape, f32),
+            jax.ShapeDtypeStruct((skeleton, columns), f32),
+        ),
+        in_specs=[anywhere] * 2,
+        out_specs=(anywhere, anywhere),
+        scratch_shapes=[dma((2,))],
+        compiler_params=pltpu.CompilerParams(vmem_limit_bytes=2**20),
+    )(updated, panel)
 
 
 def solution(mesh):

time: 29.3 us -> 28.3 us (0.966)
  local copies, waits for them, and re-layouts: 1.52 us -> 0 us
  Pallas kernels: 27 us -> 27.5 us
    unnamed x2 -> x0, local copies, waits for them, and re-layouts: 1.52 us -> none
    pallas_call x0 -> x1, Pallas kernels: none -> 0.92 us  [body(): pl.pallas_call(store, name='store', out_shape=(jax.ShapeDtypeStruct(block...]
    pallas_call x1, Pallas kernels: 27 us -> 26.6 us  [body(): pl.pallas_call(functools.partial(kernel, n_surf, n_pair), name='eliminate...]
where the time goes in v3:
time: 28.3 us; the launch traced here: 28.2 us
  Pallas kernels  27.5 us (97%)
  between operations  0.64 us (2%)
    pallas_call x1, Pallas kernels, body(): pl.pallas_call(functools.partial(kernel, n_surf, n_pair), name='eliminate...  26.6 us
    pallas_call x1, Pallas kernels, body(): pl.pallas_call(store, name='store', out_shape=(jax.ShapeDtypeStruct(block...  0.92 us

profile of v3, /device:TPU:2, one launch (start us, length us, event | category | flops | bytes accessed | tf_op | source)
XLA Modules:
  0.0 28.2 jit_solution(7317996449993423046)
XLA Ops:
  0.6 26.6 %eliminate.1 = (f32[4,192,192]{2,1,0:T(8,128)S(1)}, f32[192,128]{1,0:T(8,128)S(1)}) custom-call(s32[2,4,4]{2,1,0:T(4,128)} %target.1, bf16[2,4,192,128]{3,2,1,0:T(8,128)(2,1)} %bitcast.2, bf16[2,4,192,128]{3,2,1,0:T(8,128)(2,1)} %bitcast.3, bf16[2,128,128]{2,1,0:T(8,128)(2,1)} %inverse.1, f32[4,192,192]{2,1,0:T(8,128)} %blocks.1, bf16[16,192,128]{2,1,0:T(8,128)(2,1)} %weights.1), custom_call_target="tpu_custom_call" | custom-call | tf_op jit(solution)/shard_map/eliminate/pallas_call | solution.py:287
  27.3 0.9 %store.1 = (f32[4,192,192]{2,1,0:T(8,128)}, f32[192,128]{1,0:T(8,128)}) custom-call(f32[4,192,192]{2,1,0:T(8,128)S(1)} %get-tuple-element.4.updated, f32[192,128]{1,0:T(8,128)S(1)} %get-tuple-element.5.coarse), custom_call_target="tpu_custom_call" | custom-call | tf_op jit(solution)/shard_map/store/pallas_call | solution.py:324

commit v4 on v3

--- a/solution.py
+++ b/solution.py
@@ -75,7 +75,7 @@
     for load in loads[:4]:
         load.wait()
 
-    units = [(b, k, l) for b in range(boxes) for k in range(neighbours) for l in range(k, neighbours)]
+    units = [(b, k, l) for b in range(boxes) for l in range(neighbours) for k in range(l + 1)]
     count = len(units)
     where_to = []
     for b, k, l in units:
@@ -106,28 +106,42 @@
         for k in range(neighbours):
             mine = solved[k * skeleton : (k + 1) * skeleton]
             panel = left_v[b, k]
-            rows_a[b, k, :, :redundant] = panel
-            rows_a[b, k, :, redundant:] = mine
+            for r in range(CHUNKS):
+                rows_a[b, r, k, :, :redundant] = panel[r * rows : (r + 1) * rows]
+                rows_a[b, r, k, :, redundant:] = mine[r * rows : (r + 1) * rows]
             both = jnp.concatenate([mine, panel], axis=1)
             both = jnp.concatenate([both, both[redundant:]], axis=0)
             cols_b[b, k] = both.T
 
     lanes = lax.broadcasted_iota(jnp.int32, (half, 128), 1)
-    for u, (b, k, l) in enumerate(units):
-        if k == l:
-            unit = jnp.dot(
-                rows_a[b, k, :, :redundant], cols_b[b, l, :redundant], preferred_element_type=jnp.float32
-            )
-        else:
-            unit = jnp.dot(rows_a[b, k], cols_b[b, l], preferred_element_type=jnp.float32)
-        before = index[u]
-        for r in range(CHUNKS):
-            top = r * rows
-            at = r * packed
-            acc[u, at : at + rows] = unit[top : top + rows, :128] + acc[before, at : at + rows]
-            tail = jnp.where(lanes < 64, unit[top : top + half, 128:], unit[top + half : top + rows, 128:])
-            acc[u, at + rows : at + packed] = tail + acc[before, at + rows : at + packed]
-
+
+    def make_units(r):
+        top = r * packed
+        for b in range(boxes):
+            for l in range(neighbours):
+                found = []
+                if l > 0:
+                    stacked = jnp.dot(
+                        rows_a[b, r, :l].reshape(l * rows, 2 * redundant),
+                        cols_b[b, l],
+                        preferred_element_type=jnp.float32,
+                    )
+                    found = [stacked[k * rows : (k + 1) * rows] for k in range(l)]
+                found.append(
+                    jnp.dot(
+                        rows_a[b, r, l, :, :redundant],
+                        cols_b[b, l, :redundant],
+                        preferred_element_type=jnp.float32,
+                    )
+                )
+                for k, unit in enumerate(found):
+                    u = units.index((b, k, l))
+                    before = index[u]
+                    acc[u, top : top + rows] = unit[:, :128] + acc[before, top : top + rows]
+                    tail = jnp.where(lanes < 64, unit[:half, 128:], unit[half:, 128:])
+                    acc[u, top + rows : top + packed] = tail + acc[before, top + rows : top + packed]
+
+    make_units(0)
     pl.semaphore_wait(barrier, 2 * REACH + n_pair - 1 - late)
     greet(True)
 
@@ -158,8 +172,8 @@
             src_ref=source, dst_ref=into, send_sem=sem, recv_sem=sem, device_id=(surf, across(1)), device_id_type=MESH
         ).wait_recv()
 
-    def send(kind, r):
-        copy = pltpu.make_async_remote_copy(
+    def to_send(kind, r):
+        return pltpu.make_async_remote_copy(
             src_ref=pieces.at[kind, r],
             dst_ref=arrived.at[kind, r],
             send_sem=send_sem,
@@ -167,26 +181,33 @@
             device_id=(tile(to[kind]), pair),
             device_id_type=MESH,
         )
-        copy.start()
-        return copy
 
     copies = {}
-    for kind in (RELAY, PARTNER, FAR):
-        if kind == FAR:
-            @pl.when(surf == 0)
-            def _():
-                pl.semaphore_wait(barrier, REACH)
-
-        for r in range(CHUNKS):
+    for r in range(CHUNKS):
+        if r > 0:
+            make_units(r)
+        for kind in (RELAY, FAR, PARTNER):
             for slot in range(local):
                 pieces[kind, r, slot] = piece_of(SPOT_OF[kind], slot, r).astype(jnp.bfloat16)
-            copies[kind, r] = send(kind, r)
+            copies[kind, r] = to_send(kind, r)
+            if kind == FAR:
+                pl.when(surf != 0)(copies[kind, r].start)
+            else:
+                copies[kind, r].start()
+
+    @pl.when(surf == 0)
+    def _():
+        pl.semaphore_wait(barrier, REACH)
+        for r in range(CHUNKS):
+            copies[FAR, r].start()
+
     for r in range(CHUNKS):
         copies[RELAY, r].wait_recv()
         for slot in range(local):
             joined = piece_of(SPOT_OF[NEAR], slot, r) + arrived[RELAY, r, slot].astype(jnp.float32)
             pieces[NEAR, r, slot] = joined.astype(jnp.bfloat16)
-        copies[NEAR, r] = send(NEAR, r)
+        copies[NEAR, r] = to_send(NEAR, r)
+        copies[NEAR, r].start()
 
     loads[4].wait()
     loads[5].wait()
@@ -299,7 +320,7 @@
             pltpu.VMEM((boxes, neighbours, skeleton, redundant), bf16),
             pltpu.VMEM(inverse.shape, bf16),
             pltpu.VMEM(blocks.shape, f32),
-            pltpu.VMEM((boxes, neighbours, skeleton, 2 * redundant), bf16),
+            pltpu.VMEM((boxes, CHUNKS, neighbours, rows, 2 * redundant), bf16),
             pltpu.VMEM((boxes, neighbours, 2 * redundant, 256), bf16),
             pltpu.VMEM((count + 1, CHUNKS * packed, 128), f32),
             pltpu.SMEM((count + SPOTS * local,), jnp.int32),

time: 28.3 us -> 27.7 us (0.979)
  Pallas kernels: 27.5 us -> 27 us
    pallas_call x1, Pallas kernels: 26.6 us -> 26 us  [body(): pl.pallas_call(functools.partial(kernel, n_surf, n_pair), name='eliminate...]
where the time goes in v4:
time: 27.7 us; the launch traced here: 27.6 us
  Pallas kernels  27 us (97%)
  between operations  0.64 us (2%)
    pallas_call x1, Pallas kernels, body(): pl.pallas_call(functools.partial(kernel, n_surf, n_pair), name='eliminate...  26 us
    pallas_call x1, Pallas kernels, body(): pl.pallas_call(store, name='store', out_shape=(jax.ShapeDtypeStruct(block...  0.92 us

profile of v4, /device:TPU:2, one launch (start us, length us, event | category | flops | bytes accessed | tf_op | source)
XLA Modules:
  0.0 27.6 jit_solution(6929318703414624913)
XLA Ops:
  0.6 26.0 %eliminate.1 = (f32[4,192,192]{2,1,0:T(8,128)S(1)}, f32[192,128]{1,0:T(8,128)S(1)}) custom-call(s32[2,4,4]{2,1,0:T(4,128)} %target.1, bf16[2,4,192,128]{3,2,1,0:T(8,128)(2,1)} %bitcast.2, bf16[2,4,192,128]{3,2,1,0:T(8,128)(2,1)} %bitcast.3, bf16[2,128,128]{2,1,0:T(8,128)(2,1)} %inverse.1, f32[4,192,192]{2,1,0:T(8,128)} %blocks.1, bf16[16,192,128]{2,1,0:T(8,128)(2,1)} %weights.1), custom_call_target="tpu_custom_call" | custom-call | tf_op jit(solution)/shard_map/eliminate/pallas_call | solution.py:308
  26.7 0.9 %store.1 = (f32[4,192,192]{2,1,0:T(8,128)}, f32[192,128]{1,0:T(8,128)}) custom-call(f32[4,192,192]{2,1,0:T(8,128)S(1)} %get-tuple-element.4.updated, f32[192,128]{1,0:T(8,128)S(1)} %get-tuple-element.5.coarse), custom_call_target="tpu_custom_call" | custom-call | tf_op jit(solution)/shard_map/store/pallas_call | solution.py:345

commit v5 on v4

--- a/solution.py
+++ b/solution.py
@@ -21,7 +21,7 @@
     n_surf, n_pair, target, left, right, inverse, blocks, weights, updated, coarse,
     target_s, left_v, right_v, inverse_v, blocks_v, rows_a, cols_b, acc, index, pieces, arrived,
     weights_own, weights_in, rounded, part, part_in,
-    load_sem, send_sem, partner_sem, recv_sem, wsend_sem, wrecv_sem, psend_sem, precv_sem,
+    load_sem, send_sem, relay_sem, recv_sem, wsend_sem, wrecv_sem, psend_sem, precv_sem,
 ):
     boxes, neighbours, skeleton, redundant = left.shape
     local = blocks.shape[0]
@@ -177,7 +177,7 @@
             src_ref=pieces.at[kind, r],
             dst_ref=arrived.at[kind, r],
             send_sem=send_sem,
-            recv_sem=partner_sem if kind == PARTNER else recv_sem.at[kind, r],
+            recv_sem=relay_sem.at[r] if kind == RELAY else recv_sem.at[r],
             device_id=(tile(to[kind]), pair),
             device_id_type=MESH,
         )
@@ -214,10 +214,8 @@
     own = []
     for r in range(CHUNKS):
         top = r * rows
-        if r == 0:
-            all_in(pieces.at[PARTNER], arrived.at[PARTNER], partner_sem)
-        for kind in (FAR, NEAR):
-            copies[kind, r].wait_recv()
+        others = pl.ds(PARTNER, 3)
+        all_in(pieces.at[others, r], arrived.at[others, r], recv_sem.at[r])
         for slot in range(local):
             total = piece_of(OWN_SPOT, slot, r)
             for kind in (PARTNER, FAR, NEAR):
@@ -236,11 +234,12 @@
         def weights_of(offset, slot):
             return weights_own[slot] if offset == 0 else weights_in[(offset - 1) * local + slot]
 
-        def panel_of(first, second):
+        def panel_of(*offsets):
             total = None
             for slot in range(local):
-                both = jnp.concatenate([weights_of(first, slot), weights_of(second, slot)], axis=1)
-                term = jnp.dot(rounded[slot], both, preferred_element_type=jnp.float32)
+                factor = [weights_of(offset, slot) for offset in offsets]
+                factor = jnp.concatenate(factor, axis=1) if len(factor) > 1 else factor[0]
+                term = jnp.dot(rounded[slot], factor, preferred_element_type=jnp.float32)
                 total = term if total is None else total + term
             return total
 
@@ -257,12 +256,11 @@
             )
             copy.start()
 
-        panel = panel_of(2, 1)
-        send_part(2, panel[:, :128])
-        send_part(1, panel[:, 128:])
-        panel = panel_of(3, 0)
-        send_part(3, panel[:, :128])
-        coarse[top : top + rows] = panel[:, 128:]
+        send_part(2, panel_of(2))
+        panel = panel_of(1, 3)
+        send_part(1, panel[:, :128])
+        send_part(3, panel[:, 128:])
+        coarse[top : top + rows] = panel_of(0)
 
     all_in(part, part_in, precv_sem)
     for r in range(CHUNKS):
@@ -333,8 +331,8 @@
             pltpu.VMEM((n_pair - 1, CHUNKS, rows, columns), bf16),
             dma((6,)),
             dma,
-            dma,
-            dma((4, CHUNKS)),
+            dma((CHUNKS,)),
+            dma((CHUNKS,)),
             dma,
             dma,
             dma,

time: 27.7 us -> 27.7 us (level)
  no operation moved by 1% of the time
where the time goes in v5:
time: 27.7 us; the launch traced here: 27.5 us
  Pallas kernels  26.9 us (97%)
  between operations  0.64 us (2%)
    pallas_call x1, Pallas kernels, body(): pl.pallas_call(functools.partial(kernel, n_surf, n_pair), name='eliminate...  26 us
    pallas_call x1, Pallas kernels, body(): pl.pallas_call(store, name='store', out_shape=(jax.ShapeDtypeStruct(block...  0.92 us

profile of v5, /device:TPU:2, one launch (start us, length us, event | category | flops | bytes accessed | tf_op | source)
XLA Modules:
  0.0 27.5 jit_solution(12725243291001347500)
XLA Ops:
  0.6 26.0 %eliminate.1 = (f32[4,192,192]{2,1,0:T(8,128)S(1)}, f32[192,128]{1,0:T(8,128)S(1)}) custom-call(s32[2,4,4]{2,1,0:T(4,128)} %target.1, bf16[2,4,192,128]{3,2,1,0:T(8,128)(2,1)} %bitcast.2, bf16[2,4,192,128]{3,2,1,0:T(8,128)(2,1)} %bitcast.3, bf16[2,128,128]{2,1,0:T(8,128)(2,1)} %inverse.1, f32[4,192,192]{2,1,0:T(8,128)} %blocks.1, bf16[16,192,128]{2,1,0:T(8,128)(2,1)} %weights.1), custom_call_target="tpu_custom_call" | custom-call | tf_op jit(solution)/shard_map/eliminate/pallas_call | solution.py:306
  26.6 0.9 %store.1 = (f32[4,192,192]{2,1,0:T(8,128)}, f32[192,128]{1,0:T(8,128)}) custom-call(f32[4,192,192]{2,1,0:T(8,128)S(1)} %get-tuple-element.4.updated, f32[192,128]{1,0:T(8,128)S(1)} %get-tuple-element.5.coarse), custom_call_target="tpu_custom_call" | custom-call | tf_op jit(solution)/shard_map/store/pallas_call | solution.py:343

commit v6 on v5

--- a/solution.py
+++ b/solution.py
@@ -109,9 +109,8 @@
             for r in range(CHUNKS):
                 rows_a[b, r, k, :, :redundant] = panel[r * rows : (r + 1) * rows]
                 rows_a[b, r, k, :, redundant:] = mine[r * rows : (r + 1) * rows]
-            both = jnp.concatenate([mine, panel], axis=1)
-            both = jnp.concatenate([both, both[redundant:]], axis=0)
-            cols_b[b, k] = both.T
+            cols_b[b, k, :redundant] = jnp.concatenate([mine, mine[128:]], axis=0).T
+            cols_b[b, k, redundant:] = jnp.concatenate([panel, panel[128:]], axis=0).T
 
     lanes = lax.broadcasted_iota(jnp.int32, (half, 128), 1)
 

time: 27.7 us -> 27.7 us (level)
  no operation moved by 1% of the time
where the time goes in v6:
time: 27.7 us; the launch traced here: 27.5 us
  Pallas kernels  26.9 us (97%)
  between operations  0.64 us (2%)
    pallas_call x1, Pallas kernels, body(): pl.pallas_call(functools.partial(kernel, n_surf, n_pair), name='eliminate...  26 us
    pallas_call x1, Pallas kernels, body(): pl.pallas_call(store, name='store', out_shape=(jax.ShapeDtypeStruct(block...  0.92 us

profile of v6, /device:TPU:2, one launch (start us, length us, event | category | flops | bytes accessed | tf_op | source)
XLA Modules:
  0.0 27.5 jit_solution(12725243291001347500)
XLA Ops:
  0.6 26.0 %eliminate.1 = (f32[4,192,192]{2,1,0:T(8,128)S(1)}, f32[192,128]{1,0:T(8,128)S(1)}) custom-call(s32[2,4,4]{2,1,0:T(4,128)} %target.1, bf16[2,4,192,128]{3,2,1,0:T(8,128)(2,1)} %bitcast.2, bf16[2,4,192,128]{3,2,1,0:T(8,128)(2,1)} %bitcast.3, bf16[2,128,128]{2,1,0:T(8,128)(2,1)} %inverse.1, f32[4,192,192]{2,1,0:T(8,128)} %blocks.1, bf16[16,192,128]{2,1,0:T(8,128)(2,1)} %weights.1), custom_call_target="tpu_custom_call" | custom-call | tf_op jit(solution)/shard_map/eliminate/pallas_call | solution.py:305
  26.6 0.9 %store.1 = (f32[4,192,192]{2,1,0:T(8,128)}, f32[192,128]{1,0:T(8,128)}) custom-call(f32[4,192,192]{2,1,0:T(8,128)S(1)} %get-tuple-element.4.updated, f32[192,128]{1,0:T(8,128)S(1)} %get-tuple-element.5.coarse), custom_call_target="tpu_custom_call" | custom-call | tf_op jit(solution)/shard_map/store/pallas_call | solution.py:342
